TPU v7x, 32 devices: a whole 2x2x4 slice. The times are simulated.
32 devices in a mesh: blk: 8 (over z, y), layer: 4 (over x, core).
Axes of the slice: x: 2, y: 2, z: 4, core: 2. Of those that a mesh axis runs over, the one named last changes fastest.
Arguments:
- leaf_area: float32 [12, 16, 1024], P(None, 'layer', 'blk'), may hold values from 0 to 6
- soil_water: float32 [10, 1024], P(None, 'blk'), may hold values from 0.05 to 0.5
- root_share: float32 [16, 10], P('layer'), may hold values from 0 to 0.3
- patch_weight: float32 [16, 32768], P('layer', 'blk'), may hold values from 0 to 1
- patch_owner: int32 [32768, 1], P('blk'), may hold values from 0 to 7; in each aligned block of 4096 rows (0 to 4095, 4096 to 8191, ...) at most 1024 rows name the same one
- patch_local: int32 [32768], P('blk'), may hold values from 0 to 127
- month: int32 [1], replicated, may hold values from 0 to 11
- mix: float32 [1], replicated, may hold values from 0.1 to 0.9
Outputs:
- canopy_share: float32 [16, 1024], P('layer', 'blk')
Inputs may be any that keep to these rules, and one draw needn't show every extreme that they name: `patch_owner`: among the rows of one device, no owner is named more than 1024 times, a bound that some block reaches.
All inputs are finite; a program needn't handle non-finite values.
Results may differ from a plain program's by a relative error of at most 0.000065.
Values sent between devices are 32-bit elements; how exact they have to be, the bound alone decides.
A program may use at most 64 MiB of HBM per device.

v0:
```python
import jax
import jax.numpy as jnp
from jax import lax
from jax.sharding import PartitionSpec as P


def interpolate(leaf_area, month, mix):
    earlier_index = month[0]
    second = (earlier_index + 1) % leaf_area.shape[0]
    earlier = lax.dynamic_index_in_dim(leaf_area, earlier_index, 0, keepdims=False)
    later = lax.dynamic_index_in_dim(leaf_area, second, 0, keepdims=False)
    return mix[0] * earlier + (1.0 - mix[0]) * later


def canopy_terms(patch_weight, patch_leaf, patch_soil, root_share):
    stress = jnp.dot(root_share, patch_soil, precision=lax.Precision.HIGHEST)
    return patch_weight * (1.0 - jnp.exp(-0.5 * patch_leaf)) * stress


def exact_dot(left, right):
    return jnp.dot(left, right, precision=lax.Precision.HIGHEST)


def on_device(
    leaf_area, soil_water, root_share, patch_weight, patch_owner, patch_local, month, mix
):
    months_count, types_here, cells_here = leaf_area.shape
    patch_count = patch_local.shape[0]
    owners = patch_owner[:, 0]
    cell_iota = jnp.arange(cells_here, dtype=jnp.int32)
    devices = lax.axis_size("blk")
    capacity = max(2, 2 * patch_count // devices)
    owner_table = (owners[:, None] == jnp.arange(devices, dtype=jnp.int32)[None, :]).astype(
        jnp.float32
    )
    patch_iota = jnp.arange(patch_count, dtype=jnp.int32)
    earlier = (patch_iota[:, None] > patch_iota[None, :]).astype(jnp.float32)
    before = exact_dot(earlier, owner_table)
    ranks = jnp.sum(before * owner_table, axis=1).astype(jnp.int32)
    slots = owners * capacity + ranks
    slot_iota = jnp.arange(devices * capacity, dtype=jnp.int32)
    slot_table = (slots[:, None] == slot_iota[None, :]).astype(jnp.float32)
    packed = jnp.concatenate([patch_weight, patch_local.astype(jnp.float32)[None, :]], axis=0)
    buffer = exact_dot(packed, slot_table)
    received = lax.all_to_all(buffer, "blk", split_axis=1, concat_axis=1, tiled=True)
    weights = received[:types_here]
    cell_ids = received[types_here].astype(jnp.int32)
    cell_table = (cell_iota[:, None] == cell_ids[None, :]).astype(jnp.float32)
    current = interpolate(leaf_area, month, mix)
    patch_leaf = exact_dot(current, cell_table)
    patch_soil = exact_dot(soil_water, cell_table)
    canopy = canopy_terms(weights, patch_leaf, patch_soil, root_share)
    grid_sum = exact_dot(canopy, cell_table.T)
    total = lax.psum(jnp.sum(grid_sum, axis=0), "layer")
    return grid_sum / (1.0 + total)


def solution(mesh):
    in_specs = (
        P(None, "layer", "blk"),
        P(None, "blk"),
        P("layer", None),
        P("layer", "blk"),
        P("blk", None),
        P("blk"),
        P(),
        P(),
    )
    out_specs = P("layer", "blk")
    return jax.shard_map(
        on_device, mesh=mesh, in_specs=in_specs, out_specs=out_specs, check_vma=False
    )
```

profile of v0, /device:TPU:0, one launch (start us, length us, event | category | flops | bytes accessed | tf_op | source)
XLA Modules:
  0.0 88.4 jit_solution(17370040293893275652)
XLA Ops:
  0.0 0.0 copy-start
  0.0 0.7 convert_element_type.30
  0.7 0.0 copy-start.2
  0.7 0.0 copy-start.1
  0.7 15.9 %fusion.13 = f32[4096]{0:T(1024)S(1)} fusion(s32[4096]{0:T(1024)} %bitcast.33), kind=kOutput, calls=%fused_computation.18 | convolution fusion | flops 285339648 | bytes 32768 | tf_op jit(solution)/shard_map/dot_general | solution.py:21
  16.7 0.0 copy-done.2
  16.7 0.0 copy-done.1
  16.7 43.1 %fusion = f32[5,8192]{1,0:T(8,128)} fusion(s32[4096]{0:T(1024)S(1)} %bitcast.34, f32[5,4096]{1,0:T(8,128)S(1)} %fusion.36), kind=kOutput, calls=%fused_computation.1 | convolution fusion | flops 2046820352 | bytes 262144 | tf_op jit(solution)/shard_map/dot_general | solution.py:21
  59.8 7.3 %all-to-all-start = ((f32[5,8,1024]{2,0,1:T(8,128)}), f32[5,8,1024]{2,0,1:T(8,128)S(1)}, u32[]{:S(2)}, u32[]{:S(2)}) async-start(f32[5,8,1024]{2,0,1:T(8,128)} %bitcast.4), calls=%async_computation | async-start | bytes 524288 | tf_op jit(solution)/shard_map/all_to_all | solution.py:45
  68.5 7.6 %all-to-all-done = f32[5,8,1024]{2,0,1:T(8,128)S(1)} async-done(((f32[5,8,1024]{2,0,1:T(8,128)}), f32[5,8,1024]{2,0,1:T(8,128)S(1)}, u32[]{:S(2)}, u32[]{:S(2)}) %all-to-all-start) | async-done | bytes 163872 | tf_op jit(solution)/shard_map/all_to_all | solution.py:45
  76.1 0.0 copy-done
  76.1 1.4 %fusion.9 = f32[8192,10]{0,1:T(8,128)S(1)} fusion(f32[10,128]{1,0:T(8,128)S(1)} %copy-done, s32[8192]{0:T(1024)S(1)} %bitcast.30), kind=kOutput, calls=%fused_computation.14 | convolution fusion | flops 126877696 | bytes 365568 | tf_op jit(solution)/shard_map/dot_general | solution.py:21
  77.6 0.0 copy-start.3
  77.6 2.1 %fusion.6 = f32[4,8192]{1,0:T(4,128)S(1)} fusion(f32[4,8192]{1,0:T(4,128)S(1)} %bitcast.27, s32[8192]{0:T(1024)S(1)} %bitcast.31, f32[12,4,128]{2,1,0:T(4,128)} %param.8, s32[]{:T(128)S(6)} %select_n.16, s32[]{:T(128)S(6)} %select_n.14, f32[]{:T(128)S(6)} %sub.10, f32[]{:T(128)} %bitcast.25), kind=kOutput, calls=%fused_computation.10 | convolution fusion | flops 51480064 | bytes 299532 | tf_op jit(solution)/shard_map/dot_general | solution.py:21
  79.7 0.0 copy-done.3
  79.7 0.4 fusion.3
  80.1 2.0 %fusion.28 = (f32[128]{0:T(128)S(1)}, f32[4,128]{1,0:T(4,128)S(1)}) fusion(f32[4,8192]{1,0:T(4,128)S(1)} %fusion.3, s32[8192]{0:T(1024)S(1)} %bitcast.32), kind=kOutput, calls=%fused_computation.38 | convolution fusion | flops 51380608 | bytes 166400 | tf_op jit(solution)/shard_map/dot_general | solution.py:21
  82.1 5.7 %psum.7 = f32[128]{0:T(128)S(1)} all-reduce(f32[128]{0:T(128)S(1)} %get-tuple-element.5), channel_id=1, replica_groups=mesh['blk'=8,'layer'=4] {'layer'}, use_global_device_ids=true, to_apply=%region_2.3 | all-reduce | flops 128 | bytes 1024 | tf_op jit(solution)/shard_map/psum | solution.py:54
  87.8 0.6 broadcast_divide_fusion
  (6 shorter events, 0.1 us)
Async XLA Ops:
  0.0 76.1 %copy-start = (f32[10,128]{1,0:T(8,128)S(1)}, f32[10,128]{1,0:T(8,128)}, u32[]{:S(2)}) copy-start(f32[10,128]{1,0:T(8,128)} %param.9) | copy-start | bytes 15364
  0.7 15.9 %copy-start.2 = (s32[4096,1]{0,1:T(1,128)S(1)}, s32[4096,1]{0,1:T(1,128)}, u32[]{:S(2)}) copy-start(s32[4096,1]{0,1:T(1,128)} %param.12) | copy-start | bytes 49156
  0.7 16.0 %copy-start.1 = (f32[4,4096]{1,0:T(4,128)S(1)}, f32[4,4096]{1,0:T(4,128)}, u32[]{:S(2)}) copy-start(f32[4,4096]{1,0:T(4,128)} %param.11) | copy-start | bytes 196612
  59.8 16.2 %all-to-all-start = ((f32[5,8,1024]{2,0,1:T(8,128)}), f32[5,8,1024]{2,0,1:T(8,128)S(1)}, u32[]{:S(2)}, u32[]{:S(2)}) async-start(f32[5,8,1024]{2,0,1:T(8,128)} %bitcast.4), calls=%async_computation | async-start | bytes 524288 | tf_op jit(solution)/shard_map/all_to_all | solution.py:45
  77.6 2.1 %copy-start.3 = (f32[4,10]{1,0:T(4,128)S(1)}, f32[4,10]{1,0:T(4,128)}, u32[]{:S(2)}) copy-start(f32[4,10]{1,0:T(4,128)} %param.10) | copy-start | bytes 484
where the time goes:
time: 88.8 us; the launch traced here: 88.4 us
  matrix products  64.9 us (73%)
  waiting for transfers between devices  7.59 us (9%)
  starting transfers between devices  7.31 us (8%)
  blocking collectives  5.67 us (6%)
  other arithmetic  1.43 us (2%)
  between operations  1.42 us (2%)
    dot_general x5, matrix products, exact_dot(): return jnp.dot(left, right, precision=lax.Precision.HIGHEST)  64.5 us
    all_to_all x1, waiting for transfers between devices, on_device(): lax.all_to_all(buffer, 'blk', split_axis=1, concat_axis=1, tiled=True)  7.59 us
    all_to_all x1, starting transfers between devices, on_device(): lax.all_to_all(buffer, 'blk', split_axis=1, concat_axis=1, tiled=True)  7.31 us
    psum x1, blocking collectives, on_device(): total = lax.psum(jnp.sum(grid_sum, axis=0), 'layer')  5.67 us
  transfers between devices with their start and end apart: 1, of which 1 were waited for; matrix products, arithmetic and copies ran while one was open for 0% of the time, Pallas kernels for 0%

commit v1 on v0

--- a/solution.py
+++ b/solution.py
@@ -42,7 +42,10 @@
     slot_table = (slots[:, None] == slot_iota[None, :]).astype(jnp.float32)
     packed = jnp.concatenate([patch_weight, patch_local.astype(jnp.float32)[None, :]], axis=0)
     buffer = exact_dot(packed, slot_table)
-    received = lax.all_to_all(buffer, "blk", split_axis=1, concat_axis=1, tiled=True)
+    received = jnp.concatenate(
+        lax.all_to_all(jnp.stack(jnp.split(buffer, lax.axis_size("blk"), axis=1)), "blk", 0, 0),
+        axis=1,
+    )
     weights = received[:types_here]
     cell_ids = received[types_here].astype(jnp.int32)
     cell_table = (cell_iota[:, None] == cell_ids[None, :]).astype(jnp.float32)

time: 88.8 us -> 92.3 us (1.039)
  local copies, waits for them, and re-layouts: 0.04 us -> 4.89 us
    unnamed x8 -> x17, local copies, waits for them, and re-layouts: 0.02 us -> 4.25 us
where the time goes in v1:
time: 92.3 us; the launch traced here: 92 us
  matrix products  64.4 us (70%)
  waiting for transfers between devices  7.59 us (8%)
  starting transfers between devices  7.31 us (8%)
  blocking collectives  5.67 us (6%)
  local copies, waits for them, and re-layouts  4.89 us (5%)
  between operations  1.44 us (2%)
    dot_general x5, matrix products, exact_dot(): return jnp.dot(left, right, precision=lax.Precision.HIGHEST)  64 us
    all_to_all x1, waiting for transfers between devices, on_device(): lax.all_to_all(jnp.stack(jnp.split(buffer, lax.axis_size('blk'), axis=1))...  7.59 us
    all_to_all x1, starting transfers between devices, on_device(): lax.all_to_all(jnp.stack(jnp.split(buffer, lax.axis_size('blk'), axis=1))...  7.31 us
    psum x1, blocking collectives, on_device(): total = lax.psum(jnp.sum(grid_sum, axis=0), 'layer')  5.67 us
    unnamed x17, local copies, waits for them, and re-layouts  4.25 us
  transfers between devices with their start and end apart: 1, of which 1 were waited for; matrix products, arithmetic and copies ran while one was open for 0% of the time, Pallas kernels for 0%

profile of v1, /device:TPU:0, one launch (start us, length us, event | category | flops | bytes accessed | tf_op | source)
XLA Modules:
  0.0 92.0 jit_solution(532935269755276976)
XLA Ops:
  0.0 0.0 copy-start
  0.0 0.0 copy-start.2
  0.0 0.0 copy-start.3
  0.0 0.0 copy-start.1
  0.0 15.9 %fusion.13 = f32[4096]{0:T(1024)S(1)} fusion(s32[4096]{0:T(1024)} %bitcast.67), kind=kOutput, calls=%fused_computation.18 | convolution fusion | flops 285339648 | bytes 32768 | tf_op jit(solution)/shard_map/dot_general | solution.py:21
  16.0 0.0 copy-done.2
  16.0 0.0 copy-done.3
  16.0 0.0 copy-done.1
  16.1 42.5 %fusion = f32[5,8192]{1,0:T(8,128)S(1)} fusion(s32[4096]{0:T(1024)S(1)} %bitcast.68, f32[5,4096]{1,0:T(8,128)S(1)} %fusion.44), kind=kOutput, calls=%fused_computation.1 | convolution fusion | flops 2046820352 | bytes 262144 | tf_op jit(solution)/shard_map/dot_general | solution.py:21
  58.6 0.6 fusion.25
  59.2 0.6 fusion.24
  59.8 0.6 fusion.23
  60.4 0.6 fusion.22
  61.0 0.6 fusion.21
  61.6 0.6 fusion.20
  62.2 0.6 fusion.19
  62.8 0.6 fusion.18
  63.4 7.3 %all-to-all-start = ((f32[8,5,1024]{2,1,0:T(8,128)}), f32[8,5,1024]{2,1,0:T(8,128)S(1)}, u32[]{:S(2)}, u32[]{:S(2)}) async-start(f32[8,5,1024]{2,1,0:T(8,128)} %fusion.18), calls=%async_computation | async-start | bytes 524288 | tf_op jit(solution)/shard_map/all_to_all | solution.py:46
  72.1 7.6 %all-to-all-done = f32[8,5,1024]{2,1,0:T(8,128)S(1)} async-done(((f32[8,5,1024]{2,1,0:T(8,128)}), f32[8,5,1024]{2,1,0:T(8,128)S(1)}, u32[]{:S(2)}, u32[]{:S(2)}) %all-to-all-start) | async-done | bytes 163872 | tf_op jit(solution)/shard_map/all_to_all | solution.py:46
  79.8 0.0 copy-done
  79.8 1.4 %fusion.9 = f32[8192,10]{0,1:T(8,128)S(1)} fusion(f32[10,128]{1,0:T(8,128)S(1)} %copy-done, s32[8192]{0:T(1024)S(1)} %bitcast.64), kind=kOutput, calls=%fused_computation.14 | convolution fusion | flops 126877696 | bytes 365568 | tf_op jit(solution)/shard_map/dot_general | solution.py:21
  81.2 0.0 copy-start.4
  81.2 2.1 %fusion.6 = f32[4,8192]{1,0:T(4,128)S(1)} fusion(f32[4,8192]{1,0:T(4,128)S(1)} %bitcast.61, s32[8192]{0:T(1024)S(1)} %bitcast.65, f32[12,4,128]{2,1,0:T(4,128)} %param.8, s32[]{:T(128)S(6)} %select_n.16, s32[]{:T(128)S(6)} %select_n.14, f32[]{:T(128)S(6)} %sub.10, f32[]{:T(128)} %bitcast.57), kind=kOutput, calls=%fused_computation.10 | convolution fusion | flops 51480064 | bytes 299532 | tf_op jit(solution)/shard_map/dot_general | solution.py:21
  83.3 0.0 copy-done.4
  83.3 0.4 fusion.3
  83.7 2.0 %fusion.36 = (f32[128]{0:T(128)S(1)}, f32[4,128]{1,0:T(4,128)S(1)}) fusion(f32[4,8192]{1,0:T(4,128)S(1)} %fusion.3, s32[8192]{0:T(1024)S(1)} %bitcast.66), kind=kOutput, calls=%fused_computation.54 | convolution fusion | flops 51380608 | bytes 166400 | tf_op jit(solution)/shard_map/dot_general | solution.py:21
  85.7 5.7 %psum.7 = f32[128]{0:T(128)S(1)} all-reduce(f32[128]{0:T(128)S(1)} %get-tuple-element.5), channel_id=1, replica_groups=mesh['blk'=8,'layer'=4] {'layer'}, use_global_device_ids=true, to_apply=%region_2.3 | all-reduce | flops 128 | bytes 1024 | tf_op jit(solution)/shard_map/psum | solution.py:57
  91.4 0.6 broadcast_divide_fusion
  (7 shorter events, 0.1 us)
Async XLA Ops:
  0.0 79.8 %copy-start = (f32[10,128]{1,0:T(8,128)S(1)}, f32[10,128]{1,0:T(8,128)}, u32[]{:S(2)}) copy-start(f32[10,128]{1,0:T(8,128)} %param.9) | copy-start | bytes 15364
  0.0 16.0 %copy-start.2 = (s32[4096,1]{0,1:T(1,128)S(1)}, s32[4096,1]{0,1:T(1,128)}, u32[]{:S(2)}) copy-start(s32[4096,1]{0,1:T(1,128)} %param.12) | copy-start | bytes 49156
  0.0 16.0 %copy-start.3 = (s32[4096]{0:T(1024)S(1)}, s32[4096]{0:T(1024)}, u32[]{:S(2)}) copy-start(s32[4096]{0:T(1024)} %param.13) | copy-start | bytes 49156
  0.0 16.0 %copy-start.1 = (f32[4,4096]{1,0:T(4,128)S(1)}, f32[4,4096]{1,0:T(4,128)}, u32[]{:S(2)}) copy-start(f32[4,4096]{1,0:T(4,128)} %param.11) | copy-start | bytes 196612
  63.4 16.2 %all-to-all-start = ((f32[8,5,1024]{2,1,0:T(8,128)}), f32[8,5,1024]{2,1,0:T(8,128)S(1)}, u32[]{:S(2)}, u32[]{:S(2)}) async-start(f32[8,5,1024]{2,1,0:T(8,128)} %fusion.18), calls=%async_computation | async-start | bytes 524288 | tf_op jit(solution)/shard_map/all_to_all | solution.py:46
  81.2 2.1 %copy-start.4 = (f32[4,10]{1,0:T(4,128)S(1)}, f32[4,10]{1,0:T(4,128)}, u32[]{:S(2)}) copy-start(f32[4,10]{1,0:T(4,128)} %param.10) | copy-start | bytes 484

commit v2 on v0

--- a/solution.py
+++ b/solution.py
@@ -51,7 +51,7 @@
     patch_soil = exact_dot(soil_water, cell_table)
     canopy = canopy_terms(weights, patch_leaf, patch_soil, root_share)
     grid_sum = exact_dot(canopy, cell_table.T)
-    total = lax.psum(jnp.sum(grid_sum, axis=0), "layer")
+    total = jnp.sum(lax.all_gather(jnp.sum(grid_sum, axis=0), "layer"), axis=0)
     return grid_sum / (1.0 + total)
 
 

time: 88.8 us -> 88.2 us (level)
    psum x1 -> x0, blocking collectives: 5.67 us -> none  [on_device(): total = lax.psum(jnp.sum(grid_sum, axis=0), 'layer')]
    all_gather x0 -> x1, blocking collectives: none -> 5.06 us  [on_device(): total = jnp.sum(lax.all_gather(jnp.sum(grid_sum, axis=0), 'layer'), axis=0)]
where the time goes in v2:
time: 88.2 us; the launch traced here: 87.8 us
  matrix products  64.9 us (74%)
  waiting for transfers between devices  7.59 us (9%)
  starting transfers between devices  7.31 us (8%)
  blocking collectives  5.06 us (6%)
  other arithmetic  1.45 us (2%)
  between operations  1.42 us (2%)
    dot_general x5, matrix products, exact_dot(): return jnp.dot(left, right, precision=lax.Precision.HIGHEST)  64.5 us
    all_to_all x1, waiting for transfers between devices, on_device(): lax.all_to_all(buffer, 'blk', split_axis=1, concat_axis=1, tiled=True)  7.59 us
    all_to_all x1, starting transfers between devices, on_device(): lax.all_to_all(buffer, 'blk', split_axis=1, concat_axis=1, tiled=True)  7.31 us
    all_gather x1, blocking collectives, on_device(): total = jnp.sum(lax.all_gather(jnp.sum(grid_sum, axis=0), 'layer'), axis=0)  5.06 us
  transfers between devices with their start and end apart: 1, of which 1 were waited for; matrix products, arithmetic and copies ran while one was open for 0% of the time, Pallas kernels for 0%

profile of v2, /device:TPU:0, one launch (start us, length us, event | category | flops | bytes accessed | tf_op | source)
XLA Modules:
  0.0 87.8 jit_solution(15992603263277448623)
XLA Ops:
  0.0 0.0 copy-start
  0.0 0.7 convert_element_type.30
  0.7 0.0 copy-start.2
  0.7 0.0 copy-start.1
  0.7 15.9 %fusion.13 = f32[4096]{0:T(1024)S(1)} fusion(s32[4096]{0:T(1024)} %bitcast.34), kind=kOutput, calls=%fused_computation.18 | convolution fusion | flops 285339648 | bytes 32768 | tf_op jit(solution)/shard_map/dot_general | solution.py:21
  16.7 0.0 copy-done.2
  16.7 0.0 copy-done.1
  16.7 43.1 %fusion = f32[5,8192]{1,0:T(8,128)} fusion(s32[4096]{0:T(1024)S(1)} %bitcast.35, f32[5,4096]{1,0:T(8,128)S(1)} %fusion.36), kind=kOutput, calls=%fused_computation.1 | convolution fusion | flops 2046820352 | bytes 262144 | tf_op jit(solution)/shard_map/dot_general | solution.py:21
  59.8 7.3 %all-to-all-start = ((f32[5,8,1024]{2,0,1:T(8,128)}), f32[5,8,1024]{2,0,1:T(8,128)S(1)}, u32[]{:S(2)}, u32[]{:S(2)}) async-start(f32[5,8,1024]{2,0,1:T(8,128)} %bitcast.4), calls=%async_computation | async-start | bytes 524288 | tf_op jit(solution)/shard_map/all_to_all | solution.py:45
  68.5 7.6 %all-to-all-done = f32[5,8,1024]{2,0,1:T(8,128)S(1)} async-done(((f32[5,8,1024]{2,0,1:T(8,128)}), f32[5,8,1024]{2,0,1:T(8,128)S(1)}, u32[]{:S(2)}, u32[]{:S(2)}) %all-to-all-start) | async-done | bytes 163872 | tf_op jit(solution)/shard_map/all_to_all | solution.py:45
  76.1 0.0 copy-done
  76.1 1.4 %fusion.9 = f32[8192,10]{0,1:T(8,128)S(1)} fusion(f32[10,128]{1,0:T(8,128)S(1)} %copy-done, s32[8192]{0:T(1024)S(1)} %bitcast.31), kind=kOutput, calls=%fused_computation.14 | convolution fusion | flops 126877696 | bytes 365568 | tf_op jit(solution)/shard_map/dot_general | solution.py:21
  77.6 0.0 copy-start.3
  77.6 2.1 %fusion.6 = f32[4,8192]{1,0:T(4,128)S(1)} fusion(f32[4,8192]{1,0:T(4,128)S(1)} %bitcast.28, s32[8192]{0:T(1024)S(1)} %bitcast.32, f32[12,4,128]{2,1,0:T(4,128)} %param.8, s32[]{:T(128)S(6)} %select_n.16, s32[]{:T(128)S(6)} %select_n.14, f32[]{:T(128)S(6)} %sub.10, f32[]{:T(128)} %bitcast.26), kind=kOutput, calls=%fused_computation.10 | convolution fusion | flops 51480064 | bytes 299532 | tf_op jit(solution)/shard_map/dot_general | solution.py:21
  79.7 0.0 copy-done.3
  79.7 0.4 fusion.3
  80.1 2.0 %fusion.28 = (f32[128]{0:T(128)S(1)}, f32[4,128]{1,0:T(4,128)S(1)}) fusion(f32[4,8192]{1,0:T(4,128)S(1)} %fusion.3, s32[8192]{0:T(1024)S(1)} %bitcast.33), kind=kOutput, calls=%fused_computation.38 | convolution fusion | flops 51380608 | bytes 166400 | tf_op jit(solution)/shard_map/dot_general | solution.py:21
  82.1 5.1 %all-gather.1 = f32[4,1,128]{2,1,0:T(1,128)S(1)} all-gather(f32[1,1,128]{2,1,0:T(1,128)S(1)} %bitcast.36), channel_id=2, replica_groups=mesh['blk'=8,'layer'=4] {'layer'}, dimensions={0}, use_global_device_ids=true | all-gather | bytes 2560 | tf_op jit(solution)/shard_map/all_gather | solution.py:54
  87.2 0.6 broadcast_divide_fusion
  (7 shorter events, 0.2 us)
Async XLA Ops:
  0.0 76.1 %copy-start = (f32[10,128]{1,0:T(8,128)S(1)}, f32[10,128]{1,0:T(8,128)}, u32[]{:S(2)}) copy-start(f32[10,128]{1,0:T(8,128)} %param.9) | copy-start | bytes 15364
  0.7 15.9 %copy-start.2 = (s32[4096,1]{0,1:T(1,128)S(1)}, s32[4096,1]{0,1:T(1,128)}, u32[]{:S(2)}) copy-start(s32[4096,1]{0,1:T(1,128)} %param.12) | copy-start | bytes 49156
  0.7 16.0 %copy-start.1 = (f32[4,4096]{1,0:T(4,128)S(1)}, f32[4,4096]{1,0:T(4,128)}, u32[]{:S(2)}) copy-start(f32[4,4096]{1,0:T(4,128)} %param.11) | copy-start | bytes 196612
  59.8 16.2 %all-to-all-start = ((f32[5,8,1024]{2,0,1:T(8,128)}), f32[5,8,1024]{2,0,1:T(8,128)S(1)}, u32[]{:S(2)}, u32[]{:S(2)}) async-start(f32[5,8,1024]{2,0,1:T(8,128)} %bitcast.4), calls=%async_computation | async-start | bytes 524288 | tf_op jit(solution)/shard_map/all_to_all | solution.py:45
  77.6 2.1 %copy-start.3 = (f32[4,10]{1,0:T(4,128)S(1)}, f32[4,10]{1,0:T(4,128)}, u32[]{:S(2)}) copy-start(f32[4,10]{1,0:T(4,128)} %param.10) | copy-start | bytes 484
